TPU v7x, 32 devices: a whole 2x2x4 slice. The times are simulated.
32 devices in a mesh: frame: 4 (over x, core), rank: 8 (over z, y).
Axes of the slice: x: 2, y: 2, z: 4, core: 2. Of those that a mesh axis runs over, the one named last changes fastest.
Arguments:
- layers: float32 [4, 8, 4, 32, 16384], P('frame', 'rank')
- depth_order: int32 [4, 8], P('frame'), may hold values from 0 to 7, as said below
- tile_slots: int32 [32], replicated, may hold values from 0 to 31, each once
Outputs:
- filtered: float32 [32, 4, 4, 16384], P('frame', None, None, 'rank')
- coverage: float32 [4], P('frame')
Inputs may be any that keep to these rules, and one draw needn't show every extreme that they name: `depth_order`: each row is a permutation of the ranks in which, for every bit b, the ranks that agree on all bits from b upward take consecutive depths. `tile_slots`: slot s belongs to frame group s // 8.
All inputs are finite; a program needn't handle non-finite values.
Results may differ from a plain program's by a relative error of at most 0.00002.
Values sent between devices are 32-bit elements; how exact they have to be, the bound alone decides.
No kernel may reach another device: no remote copies, remote signals or barrier semaphores. Data moves between devices by JAX's collectives and lax.ppermute only.
A program may use at most 64 MiB of HBM per device.

v0:
```python
import jax
import jax.numpy as jnp
from jax import lax
from jax.sharding import PartitionSpec as P


def smooth_frames(block):
    before = jnp.concatenate([block[:, :, :1], block[:, :, :-1]], axis=2)
    after = jnp.concatenate([block[:, :, 1:], block[:, :, -1:]], axis=2)
    return 0.25 * before + 0.5 * block + 0.25 * after


def shards(layers, depth_order, tile_slots):
    mine = layers[0, 0]
    order = depth_order[0]
    ranks = lax.axis_size("rank")
    groups = lax.axis_size("frame")
    channels, tile_count, pixels = mine.shape
    piece = pixels // ranks
    blocks = mine.reshape(channels, tile_count, ranks, piece)
    gathered = lax.all_to_all(blocks, "rank", split_axis=2, concat_axis=2, tiled=True)

    def step(total, rank_id):
        layer = lax.dynamic_index_in_dim(gathered, rank_id, 2, keepdims=False)
        return (total + (1.0 - total[3:4]) * layer, None)

    start = jnp.zeros((gathered.shape[0], gathered.shape[1], gathered.shape[3]), jnp.float32)
    total, unused = lax.scan(step, start, order)
    opacity = lax.psum(jnp.sum(total[3]), "rank")
    coverage = (opacity / (tile_count * pixels)).reshape(1)
    picked = jnp.transpose(total[:, tile_slots, :], (1, 0, 2))
    per_group = tile_count // groups
    picked = picked.reshape(groups, per_group, 1, channels, piece)
    filtered = smooth_frames(
        lax.all_to_all(picked, "frame", split_axis=0, concat_axis=2, tiled=True)
    )
    filtered = filtered.reshape(per_group, groups, channels, piece)
    return (filtered, coverage)


def solution(mesh):
    placed = (P("frame", "rank", None, None, None), P("frame", None), P())
    return jax.shard_map(
        shards,
        mesh=mesh,
        in_specs=placed,
        out_specs=(P("frame", None, None, "rank"), P("frame")),
        check_vma=False,
    )
```

profile of v0, /device:TPU:0, one launch (start us, length us, event | category | flops | bytes accessed | tf_op | source)
XLA Modules:
  0.0 275.3 jit_solution(9798022142263179095)
XLA Ops:
  0.6 9.9 %copy.20 = f32[16,8,8,2048]{3,2,1,0:T(8,128)S(1)} copy(f32[16,8,8,2048]{3,1,2,0:T(8,128)} %bitcast.42) | data formatting | bytes 16777216
  10.5 8.1 %copy.13 = f32[4,32,8,2048]{3,1,0,2:T(8,128)} copy(f32[4,32,8,2048]{3,2,1,0:T(8,128)S(1)} %bitcast.39) | data formatting | bytes 16777216 | tf_op jit(solution)/shard_map/reshape;squeeze | solution.py:20
  18.6 0.0 copy-start
  18.6 0.0 copy-start.1
  18.6 7.6 %all-to-all-start = ((f32[4,32,8,2048]{3,1,0,2:T(8,128)}), f32[4,32,8,2048]{3,1,0,2:T(8,128)}, u32[]{:S(2)}, u32[]{:S(2)}) async-start(f32[4,32,8,2048]{3,1,0,2:T(8,128)} %copy.13), calls=%async_computation | async-start | bytes 16777216 | tf_op jit(solution)/shard_map/all_to_all | solution.py:21
  26.2 0.0 copy-done
  26.2 183.1 %all-to-all-done = f32[4,32,8,2048]{3,1,0,2:T(8,128)} async-done(((f32[4,32,8,2048]{3,1,0,2:T(8,128)}), f32[4,32,8,2048]{3,1,0,2:T(8,128)}, u32[]{:S(2)}, u32[]{:S(2)}) %all-to-all-start) | async-done | bytes 8388640 | tf_op jit(solution)/shard_map/all_to_all | solution.py:21
  209.4 0.0 copy-done.1
  209.4 34.3 %while.11 = (s32[]{:T(128)}, f32[4,32,2048]{2,1,0:T(8,128)S(1)}, s32[8]{0:T(128)S(1)}, f32[4,32,8,2048]{3,1,0,2:T(8,128)}, s32[]{:T(128)}, /*index=5*/s32[]{:T(128)}, s32[]{:T(128)}) while((s32[]{:T(128)}, f32[4,32,2048]{2,1,0:T(8,128)S(1)}, s32[8]{0:T(128)S(1)}, f32[4,32,8,2048]{3,1,0,2:T(8,128)}, s32[]{:T(128)}, ...), condition=%wide.region_1.2_spmd.clone, body=%wide.region_0.1_spmd.clone.sunk | while | flops 1114118 | bytes 6029450 | solution.py:28
  209.4 0.6 dynamic_slice.14
  211.9 0.1 broadcast_select_fusion.2
  212.0 1.6 fusion.7
  213.7 0.6 dynamic_slice.14
  216.2 0.1 broadcast_select_fusion.2
  216.3 1.6 fusion.7
  217.9 0.6 dynamic_slice.14
  220.5 0.1 broadcast_select_fusion.2
  220.6 1.6 fusion.7
  222.2 0.6 dynamic_slice.14
  224.8 0.1 broadcast_select_fusion.2
  224.9 1.6 fusion.7
  226.5 0.6 dynamic_slice.14
  229.1 0.1 broadcast_select_fusion.2
  229.2 1.6 fusion.7
  230.8 0.6 dynamic_slice.14
  233.3 0.1 broadcast_select_fusion.2
  233.5 1.6 fusion.7
  235.1 0.6 dynamic_slice.14
  237.6 0.1 broadcast_select_fusion.2
  237.8 1.6 fusion.7
  239.4 0.6 dynamic_slice.14
  241.9 0.1 broadcast_select_fusion.2
  242.1 1.6 fusion.7
  243.7 0.7 copy.14
  244.4 1.2 gather_fusion
  245.5 1.6 copy.16
  247.1 3.5 %all-to-all-start.1 = ((f32[4,8,1,4,2048]{4,1,3,2,0:T(8,128)}), f32[4,8,1,4,2048]{4,1,3,2,0:T(8,128)S(1)}, u32[]{:S(2)}, u32[]{:S(2)}) async-start(f32[4,8,1,4,2048]{4,1,3,2,0:T(8,128)} %copy.16), calls=%async_computation.1 | async-start | bytes 2097152 | tf_op jit(solution)/shard_map/all_to_all | solution.py:35
  250.6 0.7 slice_reduce_fusion
  251.3 20.1 %psum.7 = f32[]{:T(128)} all-reduce(f32[]{:T(128)} %slice_reduce_fusion), channel_id=1, replica_groups=mesh['frame'=4,'rank'=8] {'rank'}, use_global_device_ids=true, to_apply=%region_3.4 | all-reduce | flops 1 | bytes 8 | tf_op jit(solution)/shard_map/psum | solution.py:29
  272.1 0.0 all-to-all-done.1
  272.1 0.2 slice_bitcast_fusion
  272.3 0.3 fusion.3
  272.6 1.6 copy.17
  (12 shorter events, 0.2 us)
Async XLA Ops:
  18.6 7.6 %copy-start = (s32[32]{0:T(128)S(1)}, s32[32]{0:T(128)}, u32[]{:S(2)}) copy-start(s32[32]{0:T(128)} %param.7) | copy-start | bytes 388
  18.6 190.8 %copy-start.1 = (s32[1,8]{1,0:T(1,128)S(1)}, s32[1,8]{1,0:T(1,128)}, u32[]{:S(2)}) copy-start(s32[1,8]{1,0:T(1,128)} %param.6) | copy-start | bytes 100
  18.6 190.8 %all-to-all-start = ((f32[4,32,8,2048]{3,1,0,2:T(8,128)}), f32[4,32,8,2048]{3,1,0,2:T(8,128)}, u32[]{:S(2)}, u32[]{:S(2)}) async-start(f32[4,32,8,2048]{3,1,0,2:T(8,128)} %copy.13), calls=%async_computation | async-start | bytes 16777216 | tf_op jit(solution)/shard_map/all_to_all | solution.py:21
  247.1 24.9 %all-to-all-start.1 = ((f32[4,8,1,4,2048]{4,1,3,2,0:T(8,128)}), f32[4,8,1,4,2048]{4,1,3,2,0:T(8,128)S(1)}, u32[]{:S(2)}, u32[]{:S(2)}) async-start(f32[4,8,1,4,2048]{4,1,3,2,0:T(8,128)} %copy.16), calls=%async_computation.1 | async-start | bytes 2097152 | tf_op jit(solution)/shard_map/all_to_all | solution.py:35
where the time goes:
time: 276 us; the launch traced here: 275 us
  waiting for transfers between devices  183 us (66%)
  local copies, waits for them, and re-layouts  27.9 us (10%)
  blocking collectives  20.1 us (7%)
  loops' own time  15.9 us (6%)
  other arithmetic  14.7 us (5%)
  starting transfers between devices  11.1 us (4%)
    all_to_all x1, waiting for transfers between devices, shards(): lax.all_to_all(blocks, 'rank', split_axis=2, concat_axis=2, tiled=True)  183 us
    psum x1, blocking collectives, shards(): opacity = lax.psum(jnp.sum(total[3]), 'rank')  20.1 us
    another operation x1, loops' own time, shards(): total, unused = lax.scan(step, start, order)  15.9 us
    add x8, other arithmetic, step(): return (total + (1.0 - total[3:4]) * layer, None)  12.8 us
    unnamed x6, local copies, waits for them, and re-layouts  11.5 us
    another operation x1, local copies, waits for them, and re-layouts, shards(): blocks = mine.reshape(channels, tile_count, ranks, piece)  8.08 us
    all_to_all x1, starting transfers between devices, shards(): lax.all_to_all(blocks, 'rank', split_axis=2, concat_axis=2, tiled=True)  7.62 us
  transfers between devices with their start and end apart: 2, of which 1 were waited for; matrix products, arithmetic and copies ran while one was open for 0% of the time, Pallas kernels for 0%

commit v1 on v0

--- a/solution.py
+++ b/solution.py
@@ -18,7 +18,10 @@
     channels, tile_count, pixels = mine.shape
     piece = pixels // ranks
     blocks = mine.reshape(channels, tile_count, ranks, piece)
-    gathered = lax.all_to_all(blocks, "rank", split_axis=2, concat_axis=2, tiled=True)
+    size = lax.axis_size("rank")
+    pieces = jnp.stack(jnp.split(blocks, size, axis=2), axis=0)
+    pieces = lax.all_to_all(pieces, "rank", split_axis=0, concat_axis=0)
+    gathered = jnp.concatenate(pieces, axis=2)
 
     def step(total, rank_id):
         layer = lax.dynamic_index_in_dim(gathered, rank_id, 2, keepdims=False)

time: 276 us -> 295 us (1.069)
  local copies, waits for them, and re-layouts: 27.9 us -> 47.4 us
    unnamed x6 -> x14, local copies, waits for them, and re-layouts: 11.5 us -> 37 us
    another operation x1, local copies, waits for them, and re-layouts: 8.08 us -> 2.12 us  [shards(): pieces = jnp.stack(jnp.split(blocks, size, axis=2), axis=0)]
where the time goes in v1:
time: 295 us
  waiting for transfers between devices  183 us (62%)
  local copies, waits for them, and re-layouts  47.4 us (16%)
  blocking collectives  20.1 us (7%)
  loops' own time  15.9 us (5%)
  other arithmetic  14.6 us (5%)
  starting transfers between devices  11 us (4%)
    all_to_all x1, waiting for transfers between devices, shards(): pieces = lax.all_to_all(pieces, 'rank', split_axis=0, concat_axis=0)  183 us
    unnamed x14, local copies, waits for them, and re-layouts  37 us
    psum x1, blocking collectives, shards(): opacity = lax.psum(jnp.sum(total[3]), 'rank')  20.1 us
    another operation x1, loops' own time, shards(): total, unused = lax.scan(step, start, order)  15.9 us
    add x8, other arithmetic, step(): return (total + (1.0 - total[3:4]) * layer, None)  12.8 us
    all_to_all x1, starting transfers between devices, shards(): pieces = lax.all_to_all(pieces, 'rank', split_axis=0, concat_axis=0)  7.44 us
  transfers between devices with their start and end apart: 2, of which 1 were waited for; matrix products, arithmetic and copies ran while one was open for 0% of the time, Pallas kernels for 0%

profile of v1, /device:TPU:0, one launch (start us, length us, event | category | flops | bytes accessed | tf_op | source)
XLA Modules:
  0.0 294.5 jit_solution(8123978883865519611)
XLA Ops:
  0.6 9.9 %copy.26 = f32[16,8,8,2048]{3,2,1,0:T(8,128)S(1)} copy(f32[16,8,8,2048]{3,1,2,0:T(8,128)} %bitcast.86) | data formatting | bytes 16777216
  10.5 1.7 fusion.9
  12.2 2.1 fusion.8
  14.3 2.1 fusion.7
  16.5 2.1 fusion.6
  18.6 2.2 fusion.5
  20.8 2.3 fusion.4
  23.1 2.1 fusion.3
  25.2 2.1 fusion.2
  27.3 7.4 %all-to-all-start = ((f32[8,4,32,1,2048]{4,3,2,1,0:T(1,128)}), f32[8,4,32,1,2048]{4,3,2,1,0:T(1,128)}, u32[]{:S(2)}, u32[]{:S(2)}) async-start(f32[8,4,32,1,2048]{4,3,2,1,0:T(1,128)} %fusion.2), calls=%async_computation | async-start | bytes 16777216 | tf_op jit(solution)/shard_map/all_to_all | solution.py:23
  34.8 0.0 copy-done
  34.8 183.1 %all-to-all-done = f32[8,4,32,1,2048]{4,3,2,1,0:T(1,128)} async-done(((f32[8,4,32,1,2048]{4,3,2,1,0:T(1,128)}), f32[8,4,32,1,2048]{4,3,2,1,0:T(1,128)}, u32[]{:S(2)}, u32[]{:S(2)}) %all-to-all-start) | async-done | bytes 8388640 | tf_op jit(solution)/shard_map/all_to_all | solution.py:23
  217.9 10.7 %copy.28 = f32[4,32,8,1,2048]{4,1,3,0,2:T(8,128)} copy(f32[4,32,8,1,2048]{4,3,1,0,2:T(1,128)} %bitcast.9) | data formatting | bytes 16777216
  228.7 34.2 %while.11 = (s32[]{:T(128)}, f32[4,32,2048]{2,1,0:T(8,128)S(1)}, s32[8]{0:T(128)S(1)}, f32[4,32,8,2048]{3,1,0,2:T(8,128)}, s32[]{:T(128)}, /*index=5*/s32[]{:T(128)}, s32[]{:T(128)}) while((s32[]{:T(128)}, f32[4,32,2048]{2,1,0:T(8,128)S(1)}, s32[8]{0:T(128)S(1)}, f32[4,32,8,2048]{3,1,0,2:T(8,128)}, s32[]{:T(128)}, ...), condition=%wide.region_1.2_spmd.clone, body=%wide.region_0.1_spmd.clone.sunk | while | flops 1114118 | bytes 6029450 | solution.py:31
  228.7 0.6 dynamic_slice.14
  231.2 0.1 broadcast_select_fusion.2
  231.3 1.6 fusion.15
  232.9 0.6 dynamic_slice.14
  235.5 0.1 broadcast_select_fusion.2
  235.6 1.6 fusion.15
  237.2 0.6 dynamic_slice.14
  239.8 0.1 broadcast_select_fusion.2
  239.9 1.6 fusion.15
  241.5 0.6 dynamic_slice.14
  244.0 0.1 broadcast_select_fusion.2
  244.1 1.6 fusion.15
  245.8 0.6 dynamic_slice.14
  248.3 0.1 broadcast_select_fusion.2
  248.4 1.6 fusion.15
  250.0 0.6 dynamic_slice.14
  252.6 0.1 broadcast_select_fusion.2
  252.7 1.6 fusion.15
  254.3 0.6 dynamic_slice.14
  256.8 0.1 broadcast_select_fusion.2
  257.0 1.6 fusion.15
  258.6 0.6 dynamic_slice.14
  261.1 0.1 broadcast_select_fusion.2
  261.2 1.6 fusion.15
  262.8 0.7 copy.19
  263.5 1.2 gather_fusion
  264.7 1.6 copy.21
  266.3 3.5 %all-to-all-start.1 = ((f32[4,8,1,4,2048]{4,1,3,2,0:T(8,128)}), f32[4,8,1,4,2048]{4,1,3,2,0:T(8,128)S(1)}, u32[]{:S(2)}, u32[]{:S(2)}) async-start(f32[4,8,1,4,2048]{4,1,3,2,0:T(8,128)} %copy.21), calls=%async_computation.1 | async-start | bytes 2097152 | tf_op jit(solution)/shard_map/all_to_all | solution.py:38
  269.8 0.7 slice_reduce_fusion
  270.5 20.1 %psum.7 = f32[]{:T(128)} all-reduce(f32[]{:T(128)} %slice_reduce_fusion), channel_id=1, replica_groups=mesh['frame'=4,'rank'=8] {'rank'}, use_global_device_ids=true, to_apply=%region_3.4 | all-reduce | flops 1 | bytes 8 | tf_op jit(solution)/shard_map/psum | solution.py:32
  291.2 0.0 all-to-all-done.1
  291.2 0.2 slice_bitcast_fusion.8
  291.5 0.3 fusion.11
  291.7 1.6 copy.22
  (15 shorter events, 0.2 us)
Async XLA Ops:
  27.3 7.4 %copy-start = (s32[32]{0:T(128)S(1)}, s32[32]{0:T(128)}, u32[]{:S(2)}) copy-start(s32[32]{0:T(128)} %param.7) | copy-start | bytes 388
  27.3 190.6 %all-to-all-start = ((f32[8,4,32,1,2048]{4,3,2,1,0:T(1,128)}), f32[8,4,32,1,2048]{4,3,2,1,0:T(1,128)}, u32[]{:S(2)}, u32[]{:S(2)}) async-start(f32[8,4,32,1,2048]{4,3,2,1,0:T(1,128)} %fusion.2), calls=%async_computation | async-start | bytes 16777216 | tf_op jit(solution)/shard_map/all_to_all | solution.py:23
  217.9 10.7 %copy-start.1 = (s32[1,8]{1,0:T(1,128)S(1)}, s32[1,8]{1,0:T(1,128)}, u32[]{:S(2)}) copy-start(s32[1,8]{1,0:T(1,128)} %param.6) | copy-start | bytes 100
  266.3 24.9 %all-to-all-start.1 = ((f32[4,8,1,4,2048]{4,1,3,2,0:T(8,128)}), f32[4,8,1,4,2048]{4,1,3,2,0:T(8,128)S(1)}, u32[]{:S(2)}, u32[]{:S(2)}) async-start(f32[4,8,1,4,2048]{4,1,3,2,0:T(8,128)} %copy.21), calls=%async_computation.1 | async-start | bytes 2097152 | tf_op jit(solution)/shard_map/all_to_all | solution.py:38
